TPU v7x, 128 devices: a whole 4x4x4 slice. The times are simulated.
128 devices in a mesh: row: 8 (over z_lo, x), col: 16 (over y, z_hi, core).
Axes of the slice: x: 4, y: 4, z: 4 (z_hi: 2, z_lo: 2; z = z_hi * 2 + z_lo), core: 2. Of those that a mesh axis runs over, the one named last changes fastest.
Arguments:
- gate_weight: bfloat16 [4608, 36864], P('row', 'col'), may hold values from -8.838835 to 8.838835
- up_weight: bfloat16 [4608, 36864], P('row', 'col'), may hold values from -8.838835 to 8.838835
- routes: int32 [2, 8], replicated, may hold values from 0 to 7, each once within a row
Outputs:
- gate_serving: bfloat16 [4608, 36864], P('col', 'row')
- up_serving: bfloat16 [4608, 36864], P('col', 'row')
- scales: float32 [2, 36864], P(None, 'row')
Inputs may be any that keep to these rules, and one draw needn't show every extreme that they name: Each row of routes names every serving rank's piece once.
All inputs are finite; a program needn't handle non-finite values. Where the computation divides by a largest or mean magnitude, that divisor is 1e-20 or more.
Results may differ from a plain program's by a relative error of at most 0.001.
Values may be sent and summed in bfloat16 or wider, within the bound.
A program may use at most 64 MiB of HBM per device.

v0:
```python
import jax
import jax.numpy as jnp
from jax import lax
from jax.sharding import Mesh
from jax.sharding import PartitionSpec as P

COL = ("col_0", "col_1", "col_2")


EPSILON = 1e-06
LIMIT = 4.0


def copy_for_each(value, axis):
    devices = lax.axis_size(axis)
    return lax.all_to_all(
        jnp.broadcast_to(value[None], (devices, *value.shape)), axis, 0, 0, tiled=True
    )


def of_everyone(value, axis):
    everything = copy_for_each(value, axis)
    return jnp.max(everything, axis=0)


def in_one(arrays, axis):
    flat, at, outs = (jnp.concatenate([a.reshape(-1) for a in arrays]), 0, [])
    so_far = of_everyone(flat, axis)
    for a in arrays:
        outs.append(so_far[at : at + a.size].reshape(a.shape))
        at += a.size
    return tuple(outs)


def in_order(pieces, dim):
    pieces = jnp.moveaxis(pieces, 0, dim)
    lengths = pieces.shape
    return pieces.reshape(*lengths[:dim], lengths[dim] * lengths[dim + 1], *lengths[dim + 2 :])


def all_blocks(value, axes, order):
    pieces = value
    for k in order:
        pieces = lax.all_gather(pieces, axes[k])
    done = order[::-1]
    back = [done.index(k) for k in range(len(axes))]
    pieces = pieces.transpose(*back, *range(len(axes), pieces.ndim))
    return pieces.reshape(-1, *value.shape)


def gathered_by_axis(value, axes, order, dim):
    return in_order(all_blocks(value, axes, order), dim)


def column_peaks(weight):
    return jnp.max(jnp.abs(weight), axis=0).astype(jnp.float32)


def quantize(weight, peaks):
    factor = LIMIT / (peaks + EPSILON)
    return (weight.astype(jnp.float32) * factor[None, :]).astype(jnp.bfloat16)


def order_pieces(weight, order, pieces):
    height, width = weight.shape
    shaped = weight.reshape(height, pieces, width // pieces)
    return jnp.take(shaped, order, axis=1).reshape(height, width)


def own_piece(peaks, pick, pieces):
    shaped = ((peaks + EPSILON) / LIMIT).reshape(pieces, -1)
    return lax.dynamic_index_in_dim(shaped, pick, 0, keepdims=False)


def shards(gate_weight, up_weight, routes):
    pieces = lax.axis_size("row")
    row_index = lax.axis_index("row")
    gate_peaks, up_peaks = in_one((column_peaks(gate_weight), column_peaks(up_weight)), "row")
    gate_sent = order_pieces(quantize(gate_weight, gate_peaks), routes[0], pieces)
    up_sent = order_pieces(quantize(up_weight, up_peaks), routes[1], pieces)
    gate_serving, up_serving = (
        lax.all_to_all(
            lax.all_to_all(gate_sent, "row", split_axis=1, concat_axis=0, tiled=True),
            COL,
            split_axis=0,
            concat_axis=1,
            tiled=True,
        ),
        lax.all_to_all(
            lax.all_to_all(up_sent, "row", split_axis=1, concat_axis=0, tiled=True),
            COL,
            split_axis=0,
            concat_axis=1,
            tiled=True,
        ),
    )
    chosen = jnp.take(routes, row_index, axis=1)
    local_scales = jnp.stack(
        [own_piece(gate_peaks, chosen[0], pieces), own_piece(up_peaks, chosen[1], pieces)]
    )
    scales = gathered_by_axis(local_scales, COL, (1, 0, 2), 1)
    return (gate_serving, up_serving, scales)


def solution(mesh):
    finer = Mesh(
        mesh.devices.reshape(mesh.shape["row"], 4, 2, 2), ("row", "col_0", "col_1", "col_2")
    )
    return jax.shard_map(
        shards,
        mesh=finer,
        in_specs=(P("row", COL), P("row", COL), P()),
        out_specs=(P(COL, "row"), P(COL, "row"), P(None, "row")),
        check_vma=False,
    )
```

profile of v0, /device:TPU:1, one launch (start us, length us, event | category | flops | bytes accessed | tf_op | source)
XLA Modules:
  0.0 239.6 jit_solution(6475498258166576045)
XLA Ops:
  0.6 0.0 copy-start
  0.6 0.0 copy-start.2
  0.7 3.3 %abs_reduce_fusion = (bf16[2304]{0:T(1024)(128)(2,1)S(1)}, bf16[2304]{0:T(1024)(128)(2,1)S(1)}) fusion(bf16[576,2304]{1,0:T(8,128)(2,1)} %param.6, bf16[576,2304]{1,0:T(8,128)(2,1)} %param.5), kind=kLoop, calls=%fused_computation.6 | loop fusion | flops 5303808 | bytes 5317632 | tf_op jit(solution)/shard_map/reduce_max | solution.py:56
  3.9 0.7 broadcast_in_dim.25
  4.7 6.2 %all-to-all-start = ((f32[8,1,4608]{2,1,0:T(1,128)}), f32[8,1,4608]{2,1,0:T(1,128)S(1)}, u32[]{:S(2)}, u32[]{:S(2)}) async-start(f32[8,1,4608]{2,1,0:T(1,128)} %broadcast_in_dim.25), calls=%async_computation | async-start | bytes 294912 | tf_op jit(solution)/shard_map/all_to_all | solution.py:16
  10.9 0.0 copy-done.2
  10.9 0.0 copy-done
  10.9 3.0 %copy.45 = bf16[576,2304]{0,1:T(8,128)(2,1)} copy(bf16[576,2304]{1,0:T(8,128)(2,1)S(1)} %copy-done) | data formatting | bytes 5308416 | tf_op args[0]
  13.9 2.5 %all-to-all-done = f32[8,1,4608]{2,1,0:T(1,128)S(1)} async-done(((f32[8,1,4608]{2,1,0:T(1,128)}), f32[8,1,4608]{2,1,0:T(1,128)S(1)}, u32[]{:S(2)}, u32[]{:S(2)}) %all-to-all-start) | async-done | bytes 147488 | tf_op jit(solution)/shard_map/all_to_all | solution.py:16
  16.4 0.1 reduce_max.29
  16.5 0.6 fusion
  17.1 2.4 multiply_convert_fusion.1
  19.5 2.5 %gather_fusion = bf16[8,576,288]{1,2,0:T(8,128)(2,1)} fusion(bf16[576,8,288]{0,2,1:T(8,128)(2,1)S(1)} %bitcast.36, s32[1024]{0:T(1024)S(1)} %pad_clamp_fusion.1), kind=kCustom, calls=%fused_computation.clone | custom fusion | bytes 5308448 | tf_op jit(solution)/shard_map/jit(_take)/gather | solution.py:67
  22.1 3.8 %select_bitcast_fusion.1 = bf16[576,8,288]{0,2,1:T(8,128)(2,1)} fusion(bf16[8,576,288]{1,2,0:T(8,128)(2,1)} %gather_fusion, pred[8]{0:T(512)(128)(4,1)S(1)} %get-tuple-element.23), kind=kLoop, calls=%fused_computation.5 | loop fusion | flops 1327104 | bytes 5308424 | tf_op jit(solution)/shard_map/jit(_take)/select_n | solution.py:67
  25.9 0.0 copy-start.1
  25.9 4.7 %all-to-all-start.1 = ((bf16[576,8,288]{0,2,1:T(8,128)(2,1)}), bf16[576,8,288]{0,2,1:T(8,128)(2,1)}, u32[]{:S(2)}, u32[]{:S(2)}) async-start(bf16[576,8,288]{0,2,1:T(8,128)(2,1)} %select_bitcast_fusion.1), calls=%async_computation.1 | async-start | bytes 5898240 | tf_op jit(solution)/shard_map/all_to_all | solution.py:83
  30.6 0.0 copy-done.1
  30.6 3.0 %copy.50 = bf16[576,2304]{0,1:T(8,128)(2,1)} copy(bf16[576,2304]{1,0:T(8,128)(2,1)S(1)} %copy-done.1) | data formatting | bytes 5308416 | tf_op args[1]
  33.6 2.4 multiply_convert_fusion
  36.0 2.6 %gather_fusion.1 = bf16[8,576,288]{1,2,0:T(8,128)(2,1)} fusion(bf16[576,8,288]{0,2,1:T(8,128)(2,1)S(1)} %bitcast.37, s32[1024]{0:T(1024)S(1)} %pad_clamp_fusion), kind=kCustom, calls=%fused_computation.1.clone | custom fusion | bytes 5308448 | tf_op jit(solution)/shard_map/jit(_take)/gather | solution.py:67
  38.6 3.9 %select_bitcast_fusion = bf16[576,8,288]{0,2,1:T(8,128)(2,1)} fusion(bf16[8,576,288]{1,2,0:T(8,128)(2,1)} %gather_fusion.1, pred[8]{0:T(512)(128)(4,1)S(1)} %get-tuple-element.15), kind=kLoop, calls=%fused_computation.4 | loop fusion | flops 1327104 | bytes 5308424 | tf_op jit(solution)/shard_map/jit(_take)/select_n | solution.py:67
  42.4 24.4 %all-to-all-done.1 = bf16[576,8,288]{0,2,1:T(8,128)(2,1)} async-done(((bf16[576,8,288]{0,2,1:T(8,128)(2,1)}), bf16[576,8,288]{0,2,1:T(8,128)(2,1)}, u32[]{:S(2)}, u32[]{:S(2)}) %all-to-all-start.1) | async-done | bytes 2654240 | tf_op jit(solution)/shard_map/all_to_all | solution.py:83
  66.9 4.5 %all-to-all-start.3 = ((bf16[576,8,288]{0,2,1:T(8,128)(2,1)}), bf16[576,8,288]{0,2,1:T(8,128)(2,1)}, u32[]{:S(2)}, u32[]{:S(2)}) async-start(bf16[576,8,288]{0,2,1:T(8,128)(2,1)} %select_bitcast_fusion), calls=%async_computation.3 | async-start | bytes 5898240 | tf_op jit(solution)/shard_map/all_to_all | solution.py:90
  71.3 4.5 %copy.47 = bf16[8,576,288]{1,0,2:T(8,128)(2,1)} copy(bf16[8,576,288]{1,2,0:T(8,128)(2,1)} %bitcast.3) | data formatting | bytes 5308416 | tf_op jit(solution)/shard_map/all_to_all | solution.py:83
  75.8 5.4 %all_to_all.55 = bf16[16,288,288]{1,0,2:T(8,128)(2,1)S(1)} reshape(bf16[8,576,288]{1,0,2:T(8,128)(2,1)} %copy.47) | data formatting | bytes 5308416 | tf_op jit(solution)/shard_map/all_to_all | solution.py:82
  81.2 2.5 %copy.48 = bf16[16,288,288]{1,2,0:T(8,128)(2,1)} copy(bf16[16,288,288]{1,0,2:T(8,128)(2,1)S(1)} %all_to_all.55) | data formatting | bytes 5308416 | tf_op jit(solution)/shard_map/all_to_all | solution.py:82
  83.7 23.9 %all-to-all-done.3 = bf16[576,8,288]{0,2,1:T(8,128)(2,1)} async-done(((bf16[576,8,288]{0,2,1:T(8,128)(2,1)}), bf16[576,8,288]{0,2,1:T(8,128)(2,1)}, u32[]{:S(2)}, u32[]{:S(2)}) %all-to-all-start.3) | async-done | bytes 2654240 | tf_op jit(solution)/shard_map/all_to_all | solution.py:90
  107.6 8.3 %all-to-all-start.2 = ((bf16[16,288,288]{1,2,0:T(8,128)(2,1)}), bf16[16,288,288]{1,2,0:T(8,128)(2,1)S(1)}, u32[]{:S(2)}, u32[]{:S(2)}) async-start(bf16[16,288,288]{1,2,0:T(8,128)(2,1)} %copy.48), calls=%async_computation.2 | async-start | bytes 7077888 | tf_op jit(solution)/shard_map/all_to_all | solution.py:82
  115.9 4.4 %copy.51 = bf16[8,576,288]{1,0,2:T(8,128)(2,1)} copy(bf16[8,576,288]{1,2,0:T(8,128)(2,1)} %bitcast.9) | data formatting | bytes 5308416 | tf_op jit(solution)/shard_map/all_to_all | solution.py:90
  120.3 6.5 %all_to_all.61 = bf16[16,288,288]{1,0,2:T(8,128)(2,1)} reshape(bf16[8,576,288]{1,0,2:T(8,128)(2,1)} %copy.51) | data formatting | bytes 5308416 | tf_op jit(solution)/shard_map/all_to_all | solution.py:89
  126.9 4.6 %copy.52 = bf16[16,288,288]{1,2,0:T(8,128)(2,1)} copy(bf16[16,288,288]{1,0,2:T(8,128)(2,1)} %all_to_all.61) | data formatting | bytes 5308416 | tf_op jit(solution)/shard_map/all_to_all | solution.py:89
  131.4 28.8 %all-to-all-done.2 = bf16[16,288,288]{1,2,0:T(8,128)(2,1)S(1)} async-done(((bf16[16,288,288]{1,2,0:T(8,128)(2,1)}), bf16[16,288,288]{1,2,0:T(8,128)(2,1)S(1)}, u32[]{:S(2)}, u32[]{:S(2)}) %all-to-all-start.2) | async-done | bytes 2654240 | tf_op jit(solution)/shard_map/all_to_all | solution.py:82
  160.2 11.6 %all-to-all-start.4 = ((bf16[16,288,288]{1,2,0:T(8,128)(2,1)}), bf16[16,288,288]{1,2,0:T(8,128)(2,1)}, u32[]{:S(2)}, u32[]{:S(2)}) async-start(bf16[16,288,288]{1,2,0:T(8,128)(2,1)} %copy.52), calls=%async_computation.4 | async-start | bytes 7077888 | tf_op jit(solution)/shard_map/all_to_all | solution.py:89
  171.8 0.2 select_reduce_fusion
  172.0 0.6 fusion.4
  176.4 1.4 div.21
  177.8 0.7 div.19
  178.5 0.7 constant_dynamic-slice_fusion
  179.2 0.7 constant_dynamic-slice_fusion.1
  179.9 19.4 %all-gather.3 = f32[2,2,288]{2,1,0:T(2,128)S(1)} all-gather(f32[1,2,288]{2,1,0:T(2,128)S(1)} %maximum_bitcast_fusion), channel_id=2, replica_groups=mesh['row'=8,'col_0'=4,'col_1'=2,'col_2'=2] {'col_1'}, dimensions={0}, use_global_device_ids=true | all-gather | bytes 6912 | tf_op jit(solution)/shard_map/all_gather | solution.py:44
  199.3 26.1 %all-gather.1 = f32[8,2,288]{2,1,0:T(2,128)S(1)} all-gather(f32[2,2,288]{2,1,0:T(2,128)S(1)} %all-gather.3), channel_id=3, replica_groups=mesh['row'=8,'col_0'=4,'col_1'=2,'col_2'=2] {'col_0'}, dimensions={0}, use_global_device_ids=true | all-gather | bytes 23040 | tf_op jit(solution)/shard_map/all_gather | solution.py:44
  225.5 4.5 %all-gather.2 = f32[8,2,2,288]{3,2,1,0:T(2,128)S(1)} all-gather(f32[4,2,2,288]{3,2,1,0:T(2,128)S(1)} %bitcast.41), channel_id=4, replica_groups=mesh['row'=8,'col_0'=4,'col_1'=2,'col_2'=2] {'col_2'}, dimensions={0}, use_global_device_ids=true | all-gather | bytes 55296 | tf_op jit(solution)/shard_map/all_gather | solution.py:44
  230.0 0.6 copy.55
  230.6 1.5 reshape.79
  232.2 2.8 %copy.56 = bf16[288,4608]{1,0:T(8,128)(2,1)} copy(bf16[288,4608]{0,1:T(8,128)(2,1)S(1)} %bitcast.38) | data formatting | bytes 5308416 | tf_op jit(solution)/shard_map/all_to_all | solution.py:82
  235.0 0.0 all-to-all-done.4
  235.0 4.6 %copy.57 = bf16[288,4608]{1,0:T(8,128)(2,1)} copy(bf16[288,4608]{0,1:T(8,128)(2,1)} %bitcast.11) | data formatting | bytes 5308416 | tf_op jit(solution)/shard_map/all_to_all | solution.py:89
  (6 shorter events, 0.1 us)
Async XLA Ops:
  0.6 10.3 %copy-start = (bf16[576,2304]{1,0:T(8,128)(2,1)S(1)}, bf16[576,2304]{1,0:T(8,128)(2,1)}, u32[]{:S(2)}) copy-start(bf16[576,2304]{1,0:T(8,128)(2,1)} %param.5) | copy-start | bytes 7962628
  0.6 10.2 %copy-start.2 = (s32[2,8]{1,0:T(2,128)S(1)}, s32[2,8]{1,0:T(2,128)}, u32[]{:S(2)}) copy-start(s32[2,8]{1,0:T(2,128)} %param.7) | copy-start | bytes 196
  4.7 11.7 %all-to-all-start = ((f32[8,1,4608]{2,1,0:T(1,128)}), f32[8,1,4608]{2,1,0:T(1,128)S(1)}, u32[]{:S(2)}, u32[]{:S(2)}) async-start(f32[8,1,4608]{2,1,0:T(1,128)} %broadcast_in_dim.25), calls=%async_computation | async-start | bytes 294912 | tf_op jit(solution)/shard_map/all_to_all | solution.py:16
  25.9 4.7 %copy-start.1 = (bf16[576,2304]{1,0:T(8,128)(2,1)S(1)}, bf16[576,2304]{1,0:T(8,128)(2,1)}, u32[]{:S(2)}) copy-start(bf16[576,2304]{1,0:T(8,128)(2,1)} %param.6) | copy-start | bytes 7962628
  25.9 41.0 %all-to-all-start.1 = ((bf16[576,8,288]{0,2,1:T(8,128)(2,1)}), bf16[576,8,288]{0,2,1:T(8,128)(2,1)}, u32[]{:S(2)}, u32[]{:S(2)}) async-start(bf16[576,8,288]{0,2,1:T(8,128)(2,1)} %select_bitcast_fusion.1), calls=%async_computation.1 | async-start | bytes 5898240 | tf_op jit(solution)/shard_map/all_to_all | solution.py:83
  66.9 40.7 %all-to-all-start.3 = ((bf16[576,8,288]{0,2,1:T(8,128)(2,1)}), bf16[576,8,288]{0,2,1:T(8,128)(2,1)}, u32[]{:S(2)}, u32[]{:S(2)}) async-start(bf16[576,8,288]{0,2,1:T(8,128)(2,1)} %select_bitcast_fusion), calls=%async_computation.3 | async-start | bytes 5898240 | tf_op jit(solution)/shard_map/all_to_all | solution.py:90
  107.6 52.6 %all-to-all-start.2 = ((bf16[16,288,288]{1,2,0:T(8,128)(2,1)}), bf16[16,288,288]{1,2,0:T(8,128)(2,1)S(1)}, u32[]{:S(2)}, u32[]{:S(2)}) async-start(bf16[16,288,288]{1,2,0:T(8,128)(2,1)} %copy.48), calls=%async_computation.2 | async-start | bytes 7077888 | tf_op jit(solution)/shard_map/all_to_all | solution.py:82
  160.2 74.8 %all-to-all-start.4 = ((bf16[16,288,288]{1,2,0:T(8,128)(2,1)}), bf16[16,288,288]{1,2,0:T(8,128)(2,1)}, u32[]{:S(2)}, u32[]{:S(2)}) async-start(bf16[16,288,288]{1,2,0:T(8,128)(2,1)} %copy.52), calls=%async_computation.4 | async-start | bytes 7077888 | tf_op jit(solution)/shard_map/all_to_all | solution.py:89
where the time goes:
time: 241 us; the launch traced here: 240 us
  waiting for transfers between devices  79.7 us (33%)
  local copies, waits for them, and re-layouts  53.4 us (22%)
  blocking collectives  50.1 us (21%)
  starting transfers between devices  35.2 us (15%)
  other arithmetic  16.7 us (7%)
  between operations  4.63 us (2%)
    all_gather x3, blocking collectives, all_blocks(): pieces = lax.all_gather(pieces, axes[k])  50.1 us
    all_to_all x1, waiting for transfers between devices, shards(): lax.all_to_all(lax.all_to_all(gate_sent, 'row', split_axis=1, concat_axis...  28.8 us
    all_to_all x1, waiting for transfers between devices, shards(): lax.all_to_all(gate_sent, 'row', split_axis=1, concat_axis=0, tiled=True)  24.4 us
    all_to_all x1, waiting for transfers between devices, shards(): lax.all_to_all(up_sent, 'row', split_axis=1, concat_axis=0, tiled=True)  23.9 us
    all_to_all x3, local copies, waits for them, and re-layouts, shards(): lax.all_to_all(lax.all_to_all(up_sent, 'row', split_axis=1, concat_axis=0...  15.8 us
    all_to_all x1, starting transfers between devices, shards(): lax.all_to_all(lax.all_to_all(up_sent, 'row', split_axis=1, concat_axis=0...  11.6 us
    all_to_all x3, local copies, waits for them, and re-layouts, shards(): lax.all_to_all(lax.all_to_all(gate_sent, 'row', split_axis=1, concat_axis...  10.7 us
    all_to_all x1, starting transfers between devices, shards(): lax.all_to_all(lax.all_to_all(gate_sent, 'row', split_axis=1, concat_axis...  8.29 us
  transfers between devices with their start and end apart: 5, of which 4 were waited for; matrix products, arithmetic and copies ran while one was open for 17% of the time, Pallas kernels for 0%

commit v1 on v0

v1 whole, which is shorter than its diff:
```python
import functools

import jax
import jax.numpy as jnp
from jax import lax
from jax.experimental import pallas as pl
from jax.experimental.pallas import tpu as pltpu
from jax.sharding import PartitionSpec as P

MESH = pl.DeviceIdType.MESH
EPSILON = 1e-06
LIMIT = 4.0
SIDE = 288
PART = 96
PARTS = SIDE // PART
TAIL = PART // 4
ROWS = 2 * PART + TAIL
CHUNKS = 2 * PARTS


def lanes(rows):
    return lax.broadcasted_iota(jnp.int32, (rows, 128), 1)


def pack_kernel(routes, gate_ref, up_ref, out_ref, peak_ref):
    step = pl.program_id(0)

    @pl.when(step == 0)
    def _():
        peak_ref[...] = jnp.zeros_like(peak_ref)

    lane, lane_tail = lanes(PART), lanes(TAIL)
    for proj, ref in enumerate((gate_ref, up_ref)):
        for rank in range(8):
            piece = routes[proj, rank]
            start = pl.multiple_of(((9 * piece) // 4) * 128, 128)
            shift = 32 * lax.rem(piece, 4)
            back = lax.rem(128 - shift, 128)
            tiles = [
                pltpu.roll(ref[:, pl.ds(start + 128 * t, 128)].astype(jnp.float32), back, 1)
                for t in range(3)
            ]
            keep = lane < 128 - shift
            full = [jnp.where(keep, tiles[0], tiles[1]), jnp.where(keep, tiles[1], tiles[2])]
            tail = tiles[2][:TAIL]
            for g in range(1, 4):
                moved = pltpu.roll(tiles[2][g * TAIL : (g + 1) * TAIL], 32 * g, 1)
                tail = jnp.where(lane_tail < 32 * g, tail, moved)
            out_ref[rank, 0, proj, 0, :PART] = full[0].astype(jnp.bfloat16)
            out_ref[rank, 0, proj, 0, PART : 2 * PART] = full[1].astype(jnp.bfloat16)
            out_ref[rank, 0, proj, 0, 2 * PART :] = tail.astype(jnp.bfloat16)
            for t, value in enumerate((*full, tiles[2])):
                row = 3 * proj + t
                peak_ref[rank, row : row + 1] = jnp.maximum(
                    peak_ref[rank, row : row + 1],
                    jnp.max(jnp.abs(value), axis=0, keepdims=True),
                )


def pack(gate, up, routes):
    return pl.pallas_call(
        pack_kernel,
        out_shape=(
            jax.ShapeDtypeStruct((8, 2, 2, PARTS, ROWS, 128), jnp.bfloat16),
            jax.ShapeDtypeStruct((8, 8, 128), jnp.float32),
        ),
        grid_spec=pltpu.PrefetchScalarGridSpec(
            num_scalar_prefetch=1,
            grid=(2 * PARTS,),
            in_specs=[pl.BlockSpec((PART, 2304), lambda i, _: (i, 0))] * 2,
            out_specs=(
                pl.BlockSpec(
                    (8, 1, 2, 1, ROWS, 128),
                    lambda i, _: (0, i // PARTS, 0, lax.rem(i, PARTS), 0, 0),
                ),
                pl.BlockSpec((8, 8, 128), lambda i, _: (0, 0, 0)),
            ),
        ),
        compiler_params=pltpu.CompilerParams(vmem_limit_bytes=24 * 2**20),
    )(routes, gate, up)


def place():
    r, c = lax.axis_index("row"), lax.axis_index("col")
    return r % 4, c // 4, (c // 2 % 2) * 2 + r // 4, c % 2


def device(x, y, z, k):
    return ((z % 2) * 4 + x, y * 4 + (z // 2) * 2 + k)


def remote(src, dst, send, recv, to):
    return pltpu.make_async_remote_copy(
        src_ref=src, dst_ref=dst, send_sem=send, recv_sem=recv, device_id=to, device_id_type=MESH
    )


def wait_bytes(ref, sem):
    pltpu.make_async_copy(ref, ref, sem).wait()


def move_kernel(
    src, peaks, out, every, relay, mine, total, gathered, sends, relay_sems, out_sem, peak_sems
):
    x, y, z, k = place()
    z_lo, z_hi = z % 2, z // 2
    row, col = lax.axis_index("row"), lax.axis_index("col")
    goal = 2 * z_lo + x // 2
    stay = goal == y
    near = x % 2 == z_hi
    slot = goal * 4 + z_hi * 2 + k
    own = 2 * (z_lo * 4 + x) + k

    barrier = pltpu.get_barrier_semaphore()
    for n in range(1, 32):
        other = device((x + n // 8) % 4, y, (z + n // 2 % 4) % 4, (k + n % 2) % 2)
        pl.semaphore_signal(barrier, 1, device_id=other, device_id_type=MESH)
    for n in range(12):
        other = device(x, (y + 1 + n // 4) % 4, (z + 2 * (n // 2 % 2)) % 4, (k + n % 2) % 2)
        pl.semaphore_signal(barrier, 1, device_id=other, device_id_type=MESH)
    pl.semaphore_wait(barrier, 43)

    def first(dx, zl, h, p):
        xd, zd = (x + dx) % 4, 2 * (x % 2) + zl
        block = src.at[2 * (zl * 4 + xd) + h, p]
        to = device(xd, y, zd, h)
        go = jnp.logical_not(jnp.logical_and(zd == z, h == k)) if dx == 0 else None

        def both():
            @pl.when(stay)
            def _():
                remote(block, out.at[col, p], sends.at[0], out_sem, to).start()

            @pl.when(jnp.logical_not(stay))
            def _():
                remote(block, relay.at[slot, p], sends.at[0], relay_sems.at[slot, p], to).start()

        if go is None:
            both()
        else:
            pl.when(go)(both)

    def second(dy, q, p):
        yd = (y + dy) % 4
        here = yd * 4 + q
        to = device(x, yd, z, k)
        target = out.at[y * 4 + q, p]
        local = jnp.logical_and(near, jnp.logical_and(yd == goal, q == z_hi * 2 + k))

        @pl.when(local)
        def _():
            remote(src.at[own, p], target, sends.at[1], out_sem, to).start()

        @pl.when(jnp.logical_not(local))
        def _():
            wait_bytes(relay.at[here, p], relay_sems.at[here, p])
            remote(relay.at[here, p], target, sends.at[1], out_sem, to).start()

    firsts = [(dx, zl, h) for h in range(2) for zl in range(2) for dx in (2, 1, 3, 0)]
    seconds = [(dy, q) for dy in (2, 1, 3) for q in range(4)]

    def open_round(p, _):
        for f in firsts:
            first(*f, p)
        return 0

    def full_round(p, _):
        for i, f in enumerate(firsts):
            if i < len(seconds):
                second(*seconds[i], p)
            first(*f, p + 2)
        return 0

    def last_round(p, _):
        for s in seconds:
            second(*s, p)
        return 0

    lax.fori_loop(0, 1, open_round, 0)

    mine[row] = peaks[row]
    for n in range(1, 8):
        xd, zl = (x + n % 4) % 4, (z_lo + n // 4) % 2
        rank = zl * 4 + xd
        remote(
            peaks.at[rank], mine.at[row], sends.at[2], peak_sems.at[0], device(xd, y, 2 * z_hi + zl, k)
        ).start()

    keep = jnp.logical_and(near, stay)

    @pl.when(keep)
    def _():
        out[col] = src[own]

    lax.fori_loop(1, 2, open_round, 0)
    wait_bytes(mine.at[pl.ds(0, 7)], peak_sems.at[0])
    total[...] = jnp.max(mine[...], axis=0)
    lax.fori_loop(0, 1, full_round, 0)
    gathered[col] = total[...]
    for n in range(1, 16):
        yd, zd, kd = (y + n // 4) % 4, (z + 2 * (n // 2 % 2)) % 4, (k + n % 2) % 2
        remote(total, gathered.at[col], sends.at[3], peak_sems.at[1], device(x, yd, zd, kd)).start()
    lax.fori_loop(1, CHUNKS - 2, full_round, 0)
    lax.fori_loop(CHUNKS - 2, CHUNKS, last_round, 0)
    wait_bytes(gathered.at[pl.ds(0, 15)], peak_sems.at[1])
    every[...] = gathered[...]

    @pl.when(keep)
    def _():
        wait_bytes(out.at[pl.ds(0, 15)], out_sem)

    @pl.when(jnp.logical_not(keep))
    def _():
        wait_bytes(out, out_sem)

    @pl.when(near)
    def _():
        wait_bytes(src.at[pl.ds(0, 15)], sends.at[0])

    @pl.when(jnp.logical_not(near))
    def _():
        wait_bytes(src, sends.at[0])

    wait_bytes(src.at[pl.ds(0, 12)], sends.at[1])
    wait_bytes(mine.at[pl.ds(0, 7)], sends.at[2])
    wait_bytes(gathered.at[pl.ds(0, 15)], sends.at[3])


def move(blocks, peaks):
    shape = (16, CHUNKS, ROWS, 128)
    return pl.pallas_call(
        move_kernel,
        out_shape=(
            jax.ShapeDtypeStruct(shape, jnp.bfloat16),
            jax.ShapeDtypeStruct((16, 8, 128), jnp.float32),
        ),
        in_specs=[pl.BlockSpec(memory_space=pltpu.VMEM)] * 2,
        out_specs=(pl.BlockSpec(memory_space=pltpu.VMEM),) * 2,
        scratch_shapes=[
            pltpu.VMEM(shape, jnp.bfloat16),
            pltpu.VMEM((8, 8, 128), jnp.float32),
            pltpu.VMEM((8, 128), jnp.float32),
            pltpu.VMEM((16, 8, 128), jnp.float32),
            pltpu.SemaphoreType.DMA((4,)),
            pltpu.SemaphoreType.DMA((16, CHUNKS)),
            pltpu.SemaphoreType.DMA,
            pltpu.SemaphoreType.DMA((2,)),
        ],
        compiler_params=pltpu.CompilerParams(
            collective_id=0, has_side_effects=True, vmem_limit_bytes=24 * 2**20
        ),
    )(blocks.reshape(shape), peaks)


def joined(pieces, rows):
    lane = lanes(rows)
    tiles = []
    spill = None
    for i, (a, b, tail) in enumerate(pieces):
        if i:
            a, b = pltpu.roll(a, 32 * i, 1), pltpu.roll(b, 32 * i, 1)
            tiles.append(jnp.where(lane < 32 * i, spill, a))
            tiles.append(jnp.where(lane < 32 * i, a, b))
            spill = jnp.where(lane < 32 * i, b, tail)
        else:
            tiles += [a, b]
            spill = tail
    tiles.append(spill)
    return tiles


def finish_kernel(blocks, peaks, gate_ref, up_ref, scale_ref, factor):
    @pl.when(pl.program_id(0) == 0)
    def _():
        for proj in range(2):
            for quad in range(4):
                pieces = []
                for i in range(4):
                    value = peaks[4 * quad + i]
                    a, b, t = (value[3 * proj + n : 3 * proj + n + 1] for n in range(3))
                    pieces.append((a, b, pltpu.roll(t, 32 * i, 1) if i else t))
                for n, tile in enumerate(joined(pieces, 1)):
                    at = pl.ds(128 * (9 * quad + n), 128)
                    scale_ref[proj : proj + 1, at] = (tile + EPSILON) / LIMIT
                    factor[proj : proj + 1, at] = LIMIT / (tile + EPSILON)

    for proj, ref in enumerate((gate_ref, up_ref)):
        for quad in range(4):
            pieces = []
            for i in range(4):
                value = blocks[4 * quad + i, proj, 0].astype(jnp.float32)
                last = value[2 * PART :]
                tail = jnp.concatenate(
                    [pltpu.roll(last, (32 * (i - g)) % 128, 1) if i != g else last for g in range(4)],
                    axis=0,
                )
                pieces.append((value[:PART], value[PART : 2 * PART], tail))
            for n, tile in enumerate(joined(pieces, PART)):
                at = pl.ds(128 * (9 * quad + n), 128)
                ref[:, at] = (tile * factor[proj : proj + 1, at]).astype(jnp.bfloat16)


def finish(blocks, peaks):
    return pl.pallas_call(
        finish_kernel,
        out_shape=(
            jax.ShapeDtypeStruct((SIDE, 4608), jnp.bfloat16),
            jax.ShapeDtypeStruct((SIDE, 4608), jnp.bfloat16),
            jax.ShapeDtypeStruct((2, 4608), jnp.float32),
        ),
        grid=(PARTS,),
        in_specs=[
            pl.BlockSpec((16, 2, 1, ROWS, 128), lambda j: (0, 0, j, 0, 0)),
            pl.BlockSpec((16, 8, 128), lambda j: (0, 0, 0)),
        ],
        out_specs=(
            pl.BlockSpec((PART, 4608), lambda j: (j, 0)),
            pl.BlockSpec((PART, 4608), lambda j: (j, 0)),
            pl.BlockSpec((2, 4608), lambda j: (0, 0)),
        ),
        scratch_shapes=[pltpu.VMEM((2, 4608), jnp.float32)],
        compiler_params=pltpu.CompilerParams(vmem_limit_bytes=24 * 2**20),
    )(blocks.reshape(16, 2, PARTS, ROWS, 128), peaks)


def shards(gate_weight, up_weight, routes):
    return finish(*move(*pack(gate_weight, up_weight, routes)))


def solution(mesh):
    return jax.shard_map(
        shards,
        mesh=mesh,
        in_specs=(P("row", "col"), P("row", "col"), P()),
        out_specs=(P("col", "row"), P("col", "row"), P(None, "row")),
        check_vma=False,
    )
```

time: 241 us -> 124 us (0.51)
  Pallas kernels: 0 us -> 118 us
  waiting for transfers between devices: 79.7 us -> 0 us
  blocking collectives: 50.1 us -> 0 us
  local copies, waits for them, and re-layouts: 53.4 us -> 4.17 us
  starting transfers between devices: 35.2 us -> 0 us
  other arithmetic: 16.7 us -> 0 us
  between operations: 4.63 us -> 0.66 us
    pallas_call x0 -> x3, Pallas kernels: none -> 118 us  [the longest x1 105 us: move(): pl.pallas_call(move_kernel, out_shape=(jax.ShapeDtypeStruct(shape, jnp.bf...]
    all_to_all x5 -> x0, waiting for transfers between devices: 79.7 us -> none  [the longest x1 28.8 us: shards(): lax.all_to_all(lax.all_to_all(gate_sent, 'row', split_axis=1, concat_axis...]
    all_gather x3 -> x0, blocking collectives: 50.1 us -> none  [all_blocks(): pieces = lax.all_gather(pieces, axes[k])]
    all_to_all x8 -> x0, local copies, waits for them, and re-layouts: 35.3 us -> none  [the longest x3 15.8 us: shards(): lax.all_to_all(lax.all_to_all(up_sent, 'row', split_axis=1, concat_axis=0...]
    all_to_all x5 -> x0, starting transfers between devices: 35.2 us -> none  [the longest x1 11.6 us: shards(): lax.all_to_all(lax.all_to_all(up_sent, 'row', split_axis=1, concat_axis=0...]
    select_n x3 -> x0, other arithmetic: 7.88 us -> none  [the longest x2 7.7 us: order_pieces(): return jnp.take(shaped, order, axis=1).reshape(height, width)]
    gather x2 -> x0, local copies, waits for them, and re-layouts: 5.11 us -> none  [order_pieces(): return jnp.take(shaped, order, axis=1).reshape(height, width)]
    convert_element_type x2 -> x0, other arithmetic: 4.78 us -> none  [quantize(): return (weight.astype(jnp.float32) * factor[None, :]).astype(jnp.bfloat16)]
  transfers between devices with their start and end apart: 5 -> 0, of which waited for: 4 -> 0; matrix products, arithmetic and copies ran while one was open for 17% -> 0% of each run, Pallas kernels for 0% -> 0%
where the time goes in v1:
time: 124 us; the launch traced here: 123 us
  Pallas kernels  118 us (95%)
  local copies, waits for them, and re-layouts  4.17 us (3%)
    pallas_call x1, Pallas kernels, move(): pl.pallas_call(move_kernel, out_shape=(jax.ShapeDtypeStruct(shape, jnp.bf...  105 us
    pallas_call x1, Pallas kernels, pack(): pl.pallas_call(pack_kernel, out_shape=(jax.ShapeDtypeStruct((8, 2, 2, PAR...  9.02 us
    pallas_call x1, Pallas kernels, finish(): pl.pallas_call(finish_kernel, out_shape=(jax.ShapeDtypeStruct((SIDE, 4608...  4.21 us
    unnamed x6, local copies, waits for them, and re-layouts  4.17 us

profile of v1, /device:TPU:1, one launch (start us, length us, event | category | flops | bytes accessed | tf_op | source)
XLA Modules:
  0.0 123.1 jit_solution(9188167302868943605)
XLA Ops:
  0.6 0.0 copy-start
  0.6 1.7 %copy-done = bf16[576,2304]{1,0:T(8,128)(2,1)S(1)} copy-done((bf16[576,2304]{1,0:T(8,128)(2,1)S(1)}, bf16[576,2304]{1,0:T(8,128)(2,1)}, u32[]{:S(2)}) %copy-start) | copy-done | bytes 2654232
  2.4 0.0 copy-start.1
  2.4 1.7 %copy-done.1 = bf16[576,2304]{1,0:T(8,128)(2,1)S(1)} copy-done((bf16[576,2304]{1,0:T(8,128)(2,1)S(1)}, bf16[576,2304]{1,0:T(8,128)(2,1)}, u32[]{:S(2)}) %copy-start.1) | copy-done | bytes 2654232
  4.1 0.0 copy-start.2
  4.1 0.7 copy-done.2
  4.8 9.0 %shard_map.58 = (bf16[8,2,2,3,216,128]{5,4,3,2,1,0:T(8,128)(2,1)S(1)}, f32[8,8,128]{2,1,0:T(8,128)S(1)}) custom-call(s32[2,8]{1,0:T(2,128)S(1)} %copy-done.2, bf16[576,2304]{1,0:T(8,128)(2,1)S(1)} %copy-done, bf16[576,2304]{1,0:T(8,128)(2,1)S(1)} %copy-done.1), custom_call_target="tpu_custom_call" | custom-call | tf_op jit(solution)/shard_map/pallas_call | solution.py:61
  13.8 105.1 %shard_map.59 = (bf16[16,6,216,128]{3,2,1,0:T(8,128)(2,1)S(1)}, f32[16,8,128]{2,1,0:T(8,128)S(1)}) custom-call(bf16[16,6,216,128]{3,2,1,0:T(8,128)(2,1)S(1)} %bitcast.3, f32[8,8,128]{2,1,0:T(8,128)S(1)} %get-tuple-element.8.peaks), custom_call_target="tpu_custom_call" | custom-call | tf_op jit(solution)/shard_map/pallas_call | solution.py:231
  118.9 4.2 %shard_map.60 = (bf16[288,4608]{1,0:T(8,128)(2,1)}, bf16[288,4608]{1,0:T(8,128)(2,1)}, f32[2,4608]{1,0:T(2,128)}) custom-call(bf16[16,2,3,216,128]{4,3,2,1,0:T(8,128)(2,1)S(1)} %bitcast.2, f32[16,8,128]{2,1,0:T(8,128)S(1)} %get-tuple-element.10.peaks), custom_call_target="tpu_custom_call" | custom-call | tf_op jit(solution)/shard_map/pallas_call | solution.py:304
Async XLA Ops:
  0.6 1.8 %copy-start = (bf16[576,2304]{1,0:T(8,128)(2,1)S(1)}, bf16[576,2304]{1,0:T(8,128)(2,1)}, u32[]{:S(2)}) copy-start(bf16[576,2304]{1,0:T(8,128)(2,1)} %gate_ref.1) | copy-start | bytes 7962628
  2.4 1.7 %copy-start.1 = (bf16[576,2304]{1,0:T(8,128)(2,1)S(1)}, bf16[576,2304]{1,0:T(8,128)(2,1)}, u32[]{:S(2)}) copy-start(bf16[576,2304]{1,0:T(8,128)(2,1)} %up_ref.1) | copy-start | bytes 7962628
  4.1 0.7 copy-start.2

commit v2 on v0

v2 whole, which is shorter than its diff:
```python
import functools

import jax
import jax.numpy as jnp
from jax import lax
from jax.experimental import pallas as pl
from jax.experimental.pallas import tpu as pltpu
from jax.sharding import PartitionSpec as P

MESH = pl.DeviceIdType.MESH
EPSILON = 1e-06
LIMIT = 4.0
SIDE = 288
PART = 96
PARTS = SIDE // PART
TAIL = PART // 4
ROWS = 2 * PART + TAIL
CHUNKS = 2 * PARTS


def lanes(rows):
    return lax.broadcasted_iota(jnp.int32, (rows, 128), 1)


def place():
    r, c = lax.axis_index("row"), lax.axis_index("col")
    return r % 4, c // 4, (c // 2 % 2) * 2 + r // 4, c % 2


def device(x, y, z, k):
    return ((z % 2) * 4 + x, y * 4 + (z // 2) * 2 + k)


def remote(src, dst, send, recv, to):
    return pltpu.make_async_remote_copy(
        src_ref=src, dst_ref=dst, send_sem=send, recv_sem=recv, device_id=to, device_id_type=MESH
    )


def wait_bytes(ref, sem):
    pltpu.make_async_copy(ref, ref, sem).wait()


def aligned(ref, lead, piece):
    start, shift = 9 * piece // 4 * 128, 32 * (piece % 4)
    a, b, c = (
        ref[(*lead, slice(start + 128 * t, start + 128 * (t + 1)))].astype(jnp.float32) for t in range(3)
    )
    if not shift:
        return a, b, c
    a, b, c = (pltpu.roll(value, 128 - shift, 1) for value in (a, b, c))
    keep = lanes(a.shape[0]) < 128 - shift
    return jnp.where(keep, a, b), jnp.where(keep, b, c), c


def pack(routes, slab, packed, src, p):
    lane_tail = lanes(TAIL)
    for piece in range(8):
        for h in range(2):
            a, b, c = aligned(slab, (2 * p + h, slice(None)), piece)
            last = c[:TAIL]
            for g in range(1, 4):
                moved = pltpu.roll(c[g * TAIL : (g + 1) * TAIL], 32 * g, 1)
                last = jnp.where(lane_tail < 32 * g, last, moved)
            packed[2 * piece + h, :PART] = a.astype(jnp.bfloat16)
            packed[2 * piece + h, PART : 2 * PART] = b.astype(jnp.bfloat16)
            packed[2 * piece + h, 2 * PART :] = last.astype(jnp.bfloat16)
    for rank in range(8):
        piece = routes[p // PARTS, rank]
        for h in range(2):
            src[2 * rank + h, p] = packed[2 * piece + h]


def local_peaks(routes, slab, line, pieces, peaks):
    for proj in range(2):
        for at in range(0, 2304, 256):
            top = jnp.abs(slab[2 * PARTS * proj, :, at : at + 256])
            for n in range(1, 2 * PARTS):
                top = jnp.maximum(top, jnp.abs(slab[2 * PARTS * proj + n, :, at : at + 256]))
            line[proj : proj + 1, at : at + 256] = jnp.max(top.astype(jnp.float32), axis=0, keepdims=True)
    for proj in range(2):
        for piece in range(8):
            rows = aligned(line, (slice(proj, proj + 1),), piece)
            for t in range(3):
                pieces[8 * proj + piece, 3 * proj + t : 3 * proj + t + 1] = rows[t]
    upper = lax.broadcasted_iota(jnp.int32, (8, 128), 0) < 3
    for rank in range(8):
        peaks[rank] = jnp.where(upper, pieces[routes[0, rank]], pieces[8 + routes[1, rank]])


def joined(pieces, rows):
    lane = lanes(rows)
    tiles = []
    spill = None
    for i, (a, b, tail) in enumerate(pieces):
        if i:
            a, b = pltpu.roll(a, 32 * i, 1), pltpu.roll(b, 32 * i, 1)
            tiles.append(jnp.where(lane < 32 * i, spill, a))
            tiles.append(jnp.where(lane < 32 * i, a, b))
            spill = jnp.where(lane < 32 * i, b, tail)
        else:
            tiles += [a, b]
            spill = tail
    tiles.append(spill)
    return tiles


def factors(gathered, scales, factor):
    for proj in range(2):
        for quad in range(4):
            pieces = []
            for i in range(4):
                value = gathered[4 * quad + i]
                a, b, t = (value[3 * proj + n : 3 * proj + n + 1] for n in range(3))
                pieces.append((a, b, pltpu.roll(t, 32 * i, 1) if i else t))
            for n, tile in enumerate(joined(pieces, 1)):
                at = pl.ds(128 * (9 * quad + n), 128)
                scales[proj : proj + 1, at] = (tile + EPSILON) / LIMIT
                factor[proj, :, at] = LIMIT / (tile + EPSILON)


def lay_out(blocks, factor, out, p):
    proj = p // PARTS
    rows = pl.ds(pl.multiple_of((p % PARTS) * PART, PART), PART)
    for quad in range(4):
        pieces = []
        for i in range(4):
            value = blocks[4 * quad + i, p].astype(jnp.float32)
            last = value[2 * PART :]
            tail = jnp.concatenate(
                [pltpu.roll(last, (32 * (i - g)) % 128, 1) if i != g else last for g in range(4)],
                axis=0,
            )
            pieces.append((value[:PART], value[PART : 2 * PART], tail))
        for n, tile in enumerate(joined(pieces, PART)):
            at = pl.ds(128 * (9 * quad + n), 128)
            out[proj, rows, at] = (tile * factor[proj, :, at]).astype(jnp.bfloat16)


def move_kernel(
    routes, gate, up, gate_out, up_out, scales, slab, src, relay, out, final, packed, line, pieces, peaks, mine, total, gathered, factor,
    slab_sems, sends, relay_sems, out_sems, peak_sems, final_sems
):
    x, y, z, k = place()
    z_lo, z_hi = z % 2, z // 2
    row, col = lax.axis_index("row"), lax.axis_index("col")
    goal = 2 * z_lo + x // 2
    stay = goal == y
    near = x % 2 == z_hi
    slot = goal * 4 + z_hi * 2 + k
    own = 2 * (z_lo * 4 + x) + k
    keep = jnp.logical_and(near, stay)

    def slab_copy(ref, p, h):
        rows = pl.ds(h * SIDE + (p % PARTS) * PART, PART)
        return pltpu.make_async_copy(ref.at[rows], slab.at[2 * p + h], slab_sems.at[2 * p + h])

    for p in range(CHUNKS):
        for h in range(2):
            slab_copy((gate, up)[p // PARTS], p, h).start()

    barrier = pltpu.get_barrier_semaphore()
    for n in range(1, 32):
        other = device((x + n // 8) % 4, y, (z + n // 2 % 4) % 4, (k + n % 2) % 2)
        pl.semaphore_signal(barrier, 1, device_id=other, device_id_type=MESH)
    for n in range(12):
        other = device(x, (y + 1 + n // 4) % 4, (z + 2 * (n // 2 % 2)) % 4, (k + n % 2) % 2)
        pl.semaphore_signal(barrier, 1, device_id=other, device_id_type=MESH)

    def first(hi, zi, dx, p):
        h, zl = (k + hi) % 2, (z_lo + zi) % 2
        xd, zd = (x + dx) % 4, 2 * (x % 2) + zl
        block = src.at[2 * (zl * 4 + xd) + h, p]
        to = device(xd, y, zd, h)
        at_all = jnp.logical_not(near) if (hi, zi, dx) == (0, 0, 0) else True

        @pl.when(jnp.logical_and(at_all, stay))
        def _():
            remote(block, out.at[col, p], sends.at[0], out_sems.at[p], to).start()

        @pl.when(jnp.logical_and(at_all, jnp.logical_not(stay)))
        def _():
            remote(block, relay.at[slot, p], sends.at[0], relay_sems.at[slot, p], to).start()

    def second(hi, zi, a, zs, p):
        zl, ks = (z_lo + zi) % 2, (k + hi) % 2
        yd = 2 * zl + a
        q = zs * 2 + ks
        here = yd * 4 + q
        to = device(x, yd, z, k)
        target = out.at[y * 4 + q, p]
        go = yd != y
        if (hi, zi) == (0, 0):
            local = jnp.logical_and(near, jnp.logical_and(yd == goal, zs == z_hi))

            @pl.when(jnp.logical_and(go, local))
            def _():
                remote(src.at[own, p], target, sends.at[1], out_sems.at[p], to).start()

            go = jnp.logical_and(go, jnp.logical_not(local))

        @pl.when(go)
        def _():
            wait_bytes(relay.at[here, p], relay_sems.at[here, p])
            remote(relay.at[here, p], target, sends.at[1], out_sems.at[p], to).start()

    groups = [(0, 0), (0, 1), (1, 0), (1, 1)]
    firsts = [(*g, dx) for g in groups for dx in (1, 3, 2, 0)]
    seconds = [(*g, a, zs) for g in groups for a in range(2) for zs in range(2)]

    def prepare(p):
        pack(routes, slab, packed, src, p)

        @pl.when(keep)
        def _():
            out[col, p] = src[own, p]

    def full_round(p, _):
        prepare(p + 2)
        for f, s in zip(firsts, seconds):
            second(*s, p)
            first(*f, p + 2)
        return 0

    def last_round(p, _):
        for s in seconds:
            second(*s, p)
        return 0

    def result(proj, p):
        rows = pl.ds(pl.multiple_of((p % PARTS) * PART, PART), PART)
        return pltpu.make_async_copy(final.at[proj, rows], (gate_out, up_out)[proj].at[rows], final_sems.at[p])

    def arrived(p, _):
        @pl.when(keep)
        def _():
            wait_bytes(out.at[pl.ds(0, 15), p], out_sems.at[p])

        @pl.when(jnp.logical_not(keep))
        def _():
            wait_bytes(out.at[:, p], out_sems.at[p])

        lay_out(out, factor, final, p)
        for proj in range(2):
            pl.when(p // PARTS == proj)(result(proj, p).start)
        return 0

    for h in range(2):
        slab_copy(gate, 0, h).wait()
    prepare(0)
    pl.semaphore_wait(barrier, 43)
    for f in firsts:
        first(*f, 0)

    for n in range(2, 2 * CHUNKS):
        slab_copy(gate, n // 2, n % 2).wait()
    local_peaks(routes, slab, line, pieces, peaks)
    mine[row] = peaks[row]
    for n in range(1, 8):
        xd, zl = (x + n % 4) % 4, (z_lo + n // 4) % 2
        to = device(xd, y, 2 * z_hi + zl, k)
        remote(peaks.at[zl * 4 + xd], mine.at[row], sends.at[2], peak_sems.at[0], to).start()

    prepare(1)
    for f in firsts:
        first(*f, 1)
    lax.fori_loop(0, 1, full_round, 0)
    wait_bytes(mine.at[pl.ds(0, 7)], peak_sems.at[0])
    total[...] = jnp.max(mine[...], axis=0)
    gathered[col] = total[...]
    lax.fori_loop(1, 2, full_round, 0)
    for n in range(1, 4):
        to = device(x, y, (z + 2 * (n // 2)) % 4, (k + n % 2) % 2)
        remote(total, gathered.at[col], sends.at[3], peak_sems.at[1], to).start()
    lax.fori_loop(2, 3, full_round, 0)
    lax.fori_loop(3, 4, full_round, 0)
    wait_bytes(gathered.at[pl.ds(0, 3)], peak_sems.at[1])
    four = pl.ds(4 * y, 4)
    for dy in range(1, 4):
        to = device(x, (y + dy) % 4, z, k)
        remote(gathered.at[four], gathered.at[four], sends.at[4], peak_sems.at[2], to).start()
    lax.fori_loop(CHUNKS - 2, CHUNKS - 1, last_round, 0)
    lax.fori_loop(CHUNKS - 1, CHUNKS, last_round, 0)
    wait_bytes(gathered.at[pl.ds(0, 12)], peak_sems.at[2])
    factors(gathered, scales, factor)
    lax.fori_loop(0, CHUNKS, arrived, 0)

    @pl.when(near)
    def _():
        wait_bytes(src.at[pl.ds(0, 15)], sends.at[0])

    @pl.when(jnp.logical_not(near))
    def _():
        wait_bytes(src, sends.at[0])

    wait_bytes(src.at[pl.ds(0, 12)], sends.at[1])
    wait_bytes(mine.at[pl.ds(0, 7)], sends.at[2])
    wait_bytes(gathered.at[pl.ds(0, 3)], sends.at[3])
    wait_bytes(gathered.at[pl.ds(0, 12)], sends.at[4])
    for p in range(CHUNKS):
        result(p // PARTS, p).wait()


def move(gate, up, routes):
    shape = (16, CHUNKS, ROWS, 128)
    return pl.pallas_call(
        move_kernel,
        out_shape=(
            jax.ShapeDtypeStruct((SIDE, 4608), jnp.bfloat16),
            jax.ShapeDtypeStruct((SIDE, 4608), jnp.bfloat16),
            jax.ShapeDtypeStruct((2, 4608), jnp.float32),
        ),
        in_specs=[
            pl.BlockSpec(memory_space=pltpu.SMEM),
            pl.BlockSpec(memory_space=pltpu.HBM),
            pl.BlockSpec(memory_space=pltpu.HBM),
        ],
        out_specs=(
            pl.BlockSpec(memory_space=pltpu.HBM),
            pl.BlockSpec(memory_space=pltpu.HBM),
            pl.BlockSpec(memory_space=pltpu.VMEM),
        ),
        scratch_shapes=[
            pltpu.VMEM((2 * CHUNKS, PART, 2304), jnp.bfloat16),
            pltpu.VMEM(shape, jnp.bfloat16),
            pltpu.VMEM(shape, jnp.bfloat16),
            pltpu.VMEM(shape, jnp.bfloat16),
            pltpu.VMEM((2, SIDE, 4608), jnp.bfloat16),
            pltpu.VMEM((16, ROWS, 128), jnp.bfloat16),
            pltpu.VMEM((2, 2304), jnp.float32),
            pltpu.VMEM((16, 8, 128), jnp.float32),
            pltpu.VMEM((8, 8, 128), jnp.float32),
            pltpu.VMEM((8, 8, 128), jnp.float32),
            pltpu.VMEM((8, 128), jnp.float32),
            pltpu.VMEM((16, 8, 128), jnp.float32),
            pltpu.VMEM((2, 1, 4608), jnp.float32),
            pltpu.SemaphoreType.DMA((2 * CHUNKS,)),
            pltpu.SemaphoreType.DMA((5,)),
            pltpu.SemaphoreType.DMA((16, CHUNKS)),
            pltpu.SemaphoreType.DMA((CHUNKS,)),
            pltpu.SemaphoreType.DMA((3,)),
            pltpu.SemaphoreType.DMA((CHUNKS,)),
        ],
        compiler_params=pltpu.CompilerParams(
            collective_id=0, has_side_effects=True, vmem_limit_bytes=60 * 2**20
        ),
    )(routes, gate, up)


def shards(gate_weight, up_weight, routes):
    return move(gate_weight, up_weight, routes)


def solution(mesh):
    return jax.shard_map(
        shards,
        mesh=mesh,
        in_specs=(P("row", "col"), P("row", "col"), P()),
        out_specs=(P("col", "row"), P("col", "row"), P(None, "row")),
        check_vma=False,
    )
```

time: 241 us -> 85.9 us (0.36)
  waiting for transfers between devices: 79.7 us -> 0 us
  Pallas kernels: 0 us -> 78.3 us
  blocking collectives: 50.1 us -> 0 us
  local copies, waits for them, and re-layouts: 53.4 us -> 5.7 us
  starting transfers between devices: 35.2 us -> 0 us
  other arithmetic: 16.7 us -> 0 us
  between operations: 4.63 us -> 0.65 us
    all_to_all x5 -> x0, waiting for transfers between devices: 79.7 us -> none  [the longest x1 28.8 us: shards(): lax.all_to_all(lax.all_to_all(gate_sent, 'row', split_axis=1, concat_axis...]
    pallas_call x0 -> x1, Pallas kernels: none -> 78.3 us  [move(): pl.pallas_call(move_kernel, out_shape=(jax.ShapeDtypeStruct((SIDE, 4608),...]
    all_gather x3 -> x0, blocking collectives: 50.1 us -> none  [all_blocks(): pieces = lax.all_gather(pieces, axes[k])]
    all_to_all x8 -> x0, local copies, waits for them, and re-layouts: 35.3 us -> none  [the longest x3 15.8 us: shards(): lax.all_to_all(lax.all_to_all(up_sent, 'row', split_axis=1, concat_axis=0...]
    all_to_all x5 -> x0, starting transfers between devices: 35.2 us -> none  [the longest x1 11.6 us: shards(): lax.all_to_all(lax.all_to_all(up_sent, 'row', split_axis=1, concat_axis=0...]
    select_n x3 -> x0, other arithmetic: 7.88 us -> none  [the longest x2 7.7 us: order_pieces(): return jnp.take(shaped, order, axis=1).reshape(height, width)]
    gather x2 -> x0, local copies, waits for them, and re-layouts: 5.11 us -> none  [order_pieces(): return jnp.take(shaped, order, axis=1).reshape(height, width)]
    convert_element_type x2 -> x0, other arithmetic: 4.78 us -> none  [quantize(): return (weight.astype(jnp.float32) * factor[None, :]).astype(jnp.bfloat16)]
  transfers between devices with their start and end apart: 5 -> 0, of which waited for: 4 -> 0; matrix products, arithmetic and copies ran while one was open for 17% -> 0% of each run, Pallas kernels for 0% -> 0%
where the time goes in v2:
time: 85.9 us; the launch traced here: 84.6 us
  Pallas kernels  78.3 us (91%)
  local copies, waits for them, and re-layouts  5.7 us (7%)
    pallas_call x1, Pallas kernels, move(): pl.pallas_call(move_kernel, out_shape=(jax.ShapeDtypeStruct((SIDE, 4608),...  78.3 us
    unnamed x7, local copies, waits for them, and re-layouts  5.7 us

profile of v2, /device:TPU:1, one launch (start us, length us, event | category | flops | bytes accessed | tf_op | source)
XLA Modules:
  0.0 84.6 jit_solution(5217420564629468218)
XLA Ops:
  0.6 78.3 %shard_map.58 = (bf16[288,4608]{1,0:T(8,128)(2,1)}, bf16[288,4608]{1,0:T(8,128)(2,1)}, f32[2,4608]{1,0:T(2,128)}) custom-call(s32[2,8]{1,0:T(2,128)} %routes.1, bf16[576,2304]{1,0:T(8,128)(2,1)} %gate.1, bf16[576,2304]{1,0:T(8,128)(2,1)} %up.1), custom_call_target="tpu_custom_call" | custom-call | tf_op jit(solution)/shard_map/pallas_call | solution.py:306
  78.9 0.0 copy-start
  78.9 3.6 %copy.9 = bf16[288,4608]{1,0:T(8,128)(2,1)} copy(bf16[288,4608]{1,0:T(8,128)(2,1)} %get-tuple-element.6) | data formatting | bytes 5308416
  82.5 0.0 copy-done
  82.5 0.0 copy-start.1
  82.5 1.5 %copy.10 = bf16[288,4608]{1,0:T(8,128)(2,1)} copy(bf16[288,4608]{1,0:T(8,128)(2,1)S(1)} %copy-done) | data formatting | bytes 5308416
  84.0 0.0 copy-done.1
  84.0 0.6 copy.11
Async XLA Ops:
  78.9 3.6 %copy-start = (bf16[288,4608]{1,0:T(8,128)(2,1)S(1)}, bf16[288,4608]{1,0:T(8,128)(2,1)}, u32[]{:S(2)}) copy-start(bf16[288,4608]{1,0:T(8,128)(2,1)} %get-tuple-element.7) | copy-start | bytes 7962628
  82.5 1.5 %copy-start.1 = (f32[2,4608]{1,0:T(2,128)S(1)}, f32[2,4608]{1,0:T(2,128)}, u32[]{:S(2)}) copy-start(f32[2,4608]{1,0:T(2,128)} %get-tuple-element.8) | copy-start | bytes 110596

commit v3 on v2

--- a/solution.py
+++ b/solution.py
@@ -53,10 +53,10 @@
     return jnp.where(keep, a, b), jnp.where(keep, b, c), c
 
 
-def pack(routes, slab, packed, src, p):
+def pack(routes, slab, packed, src, p, halves):
     lane_tail = lanes(TAIL)
     for piece in range(8):
-        for h in range(2):
+        for h in halves:
             a, b, c = aligned(slab, (2 * p + h, slice(None)), piece)
             last = c[:TAIL]
             for g in range(1, 4):
@@ -67,7 +67,7 @@
             packed[2 * piece + h, 2 * PART :] = last.astype(jnp.bfloat16)
     for rank in range(8):
         piece = routes[p // PARTS, rank]
-        for h in range(2):
+        for h in halves:
             src[2 * rank + h, p] = packed[2 * piece + h]
 
 
@@ -138,8 +138,8 @@
 
 
 def move_kernel(
-    routes, gate, up, gate_out, up_out, scales, slab, src, relay, out, final, packed, line, pieces, peaks, mine, total, gathered, factor,
-    slab_sems, sends, relay_sems, out_sems, peak_sems, final_sems
+    routes_in, gate, up, final, scales, routes, slab, src, relay, out, packed, line, pieces, peaks, mine, total, gathered, factor,
+    slab_sems, sends, relay_sems, out_sems, peak_sems, routes_sem
 ):
     x, y, z, k = place()
     z_lo, z_hi = z % 2, z // 2
@@ -151,13 +151,16 @@
     own = 2 * (z_lo * 4 + x) + k
     keep = jnp.logical_and(near, stay)
 
-    def slab_copy(ref, p, h):
-        rows = pl.ds(h * SIDE + (p % PARTS) * PART, PART)
-        return pltpu.make_async_copy(ref.at[rows], slab.at[2 * p + h], slab_sems.at[2 * p + h])
-
-    for p in range(CHUNKS):
-        for h in range(2):
-            slab_copy((gate, up)[p // PARTS], p, h).start()
+    def slab_copy(p, h):
+        rows = pl.ds(h * SIDE + p % PARTS * PART, PART)
+        return pltpu.make_async_copy(
+            (gate, up)[p // PARTS].at[rows], slab.at[2 * p + h], slab_sems.at[2 * p + h]
+        )
+
+    routes_copy = pltpu.make_async_copy(routes_in, routes, routes_sem)
+    routes_copy.start()
+    slab_copy(0, k).start()
+    slab_copy(0, 1 - k).start()
 
     barrier = pltpu.get_barrier_semaphore()
     for n in range(1, 32):
@@ -208,15 +211,17 @@
     firsts = [(*g, dx) for g in groups for dx in (1, 3, 2, 0)]
     seconds = [(*g, a, zs) for g in groups for a in range(2) for zs in range(2)]
 
-    def prepare(p):
-        pack(routes, slab, packed, src, p)
-
+    def prepare(p, halves=(0, 1)):
+        pack(routes, slab, packed, src, p, halves)
+
+    def keep_own(p):
         @pl.when(keep)
         def _():
             out[col, p] = src[own, p]
 
     def full_round(p, _):
         prepare(p + 2)
+        keep_own(p + 2)
         for f, s in zip(firsts, seconds):
             second(*s, p)
             first(*f, p + 2)
@@ -227,10 +232,6 @@
             second(*s, p)
         return 0
 
-    def result(proj, p):
-        rows = pl.ds(pl.multiple_of((p % PARTS) * PART, PART), PART)
-        return pltpu.make_async_copy(final.at[proj, rows], (gate_out, up_out)[proj].at[rows], final_sems.at[p])
-
     def arrived(p, _):
         @pl.when(keep)
         def _():
@@ -241,19 +242,24 @@
             wait_bytes(out.at[:, p], out_sems.at[p])
 
         lay_out(out, factor, final, p)
-        for proj in range(2):
-            pl.when(p // PARTS == proj)(result(proj, p).start)
         return 0
 
-    for h in range(2):
-        slab_copy(gate, 0, h).wait()
-    prepare(0)
+    for n in range(2, 2 * CHUNKS):
+        slab_copy(n // 2, n % 2).start()
+    routes_copy.wait()
+    slab_copy(0, k).wait()
+    prepare(0, (k,))
     pl.semaphore_wait(barrier, 43)
-    for f in firsts:
+    for f in firsts[:8]:
         first(*f, 0)
+    slab_copy(0, 1 - k).wait()
+    prepare(0, (1 - k,))
+    for f in firsts[8:]:
+        first(*f, 0)
+    keep_own(0)
 
     for n in range(2, 2 * CHUNKS):
-        slab_copy(gate, n // 2, n % 2).wait()
+        slab_copy(n // 2, n % 2).wait()
     local_peaks(routes, slab, line, pieces, peaks)
     mine[row] = peaks[row]
     for n in range(1, 8):
@@ -262,6 +268,7 @@
         remote(peaks.at[zl * 4 + xd], mine.at[row], sends.at[2], peak_sems.at[0], to).start()
 
     prepare(1)
+    keep_own(1)
     for f in firsts:
         first(*f, 1)
     lax.fori_loop(0, 1, full_round, 0)
@@ -297,8 +304,6 @@
     wait_bytes(mine.at[pl.ds(0, 7)], sends.at[2])
     wait_bytes(gathered.at[pl.ds(0, 3)], sends.at[3])
     wait_bytes(gathered.at[pl.ds(0, 12)], sends.at[4])
-    for p in range(CHUNKS):
-        result(p // PARTS, p).wait()
 
 
 def move(gate, up, routes):
@@ -306,26 +311,21 @@
     return pl.pallas_call(
         move_kernel,
         out_shape=(
-            jax.ShapeDtypeStruct((SIDE, 4608), jnp.bfloat16),
-            jax.ShapeDtypeStruct((SIDE, 4608), jnp.bfloat16),
-            jax.ShapeDtypeStruct((2, 4608), jnp.float32),
+            pltpu.VMEM((2, SIDE, 4608), jnp.bfloat16),
+            pltpu.VMEM((2, 4608), jnp.float32),
         ),
         in_specs=[
-            pl.BlockSpec(memory_space=pltpu.SMEM),
+            pl.BlockSpec(memory_space=pltpu.HBM),
             pl.BlockSpec(memory_space=pltpu.HBM),
             pl.BlockSpec(memory_space=pltpu.HBM),
         ],
-        out_specs=(
-            pl.BlockSpec(memory_space=pltpu.HBM),
-            pl.BlockSpec(memory_space=pltpu.HBM),
-            pl.BlockSpec(memory_space=pltpu.VMEM),
-        ),
+        out_specs=(pl.BlockSpec(memory_space=pltpu.VMEM),) * 2,
         scratch_shapes=[
+            pltpu.SMEM((2, 8), jnp.int32),
             pltpu.VMEM((2 * CHUNKS, PART, 2304), jnp.bfloat16),
             pltpu.VMEM(shape, jnp.bfloat16),
             pltpu.VMEM(shape, jnp.bfloat16),
             pltpu.VMEM(shape, jnp.bfloat16),
-            pltpu.VMEM((2, SIDE, 4608), jnp.bfloat16),
             pltpu.VMEM((16, ROWS, 128), jnp.bfloat16),
             pltpu.VMEM((2, 2304), jnp.float32),
             pltpu.VMEM((16, 8, 128), jnp.float32),
@@ -339,16 +339,53 @@
             pltpu.SemaphoreType.DMA((16, CHUNKS)),
             pltpu.SemaphoreType.DMA((CHUNKS,)),
             pltpu.SemaphoreType.DMA((3,)),
-            pltpu.SemaphoreType.DMA((CHUNKS,)),
+            pltpu.SemaphoreType.DMA,
         ],
         compiler_params=pltpu.CompilerParams(
-            collective_id=0, has_side_effects=True, vmem_limit_bytes=60 * 2**20
+            collective_id=0, has_side_effects=True, vmem_limit_bytes=40 * 2**20
         ),
-    )(routes, gate, up)
+    )(
+        pltpu.with_memory_space_constraint(routes, pltpu.HBM),
+        pltpu.with_memory_space_constraint(gate, pltpu.HBM),
+        pltpu.with_memory_space_constraint(up, pltpu.HBM),
+    )
+
+
+def store_kernel(final, lines, gate, up, scales, sems):
+    copies = [
+        pltpu.make_async_copy(
+            final.at[proj, pl.ds(i * PART, PART)], ref.at[pl.ds(i * PART, PART)], sems.at[proj * PARTS + i]
+        )
+        for proj, ref in enumerate((gate, up))
+        for i in range(PARTS)
+    ]
+    copies.append(pltpu.make_async_copy(lines, scales, sems.at[2 * PARTS]))
+    for copy in copies:
+        copy.start()
+    for copy in copies:
+        copy.wait()
+
+
+def store(final, lines):
+    return pl.pallas_call(
+        store_kernel,
+        out_shape=(
+            jax.ShapeDtypeStruct((SIDE, 4608), jnp.bfloat16),
+            jax.ShapeDtypeStruct((SIDE, 4608), jnp.bfloat16),
+            jax.ShapeDtypeStruct((2, 4608), jnp.float32),
+        ),
+        in_specs=[pl.BlockSpec(memory_space=pltpu.VMEM)] * 2,
+        out_specs=(pl.BlockSpec(memory_space=pltpu.HBM),) * 3,
+        scratch_shapes=[pltpu.SemaphoreType.DMA((2 * PARTS + 1,))],
+        compiler_params=pltpu.CompilerParams(vmem_limit_bytes=2**20),
+    )(
+        pltpu.with_memory_space_constraint(final, pltpu.VMEM),
+        pltpu.with_memory_space_constraint(lines, pltpu.VMEM),
+    )
 
 
 def shards(gate_weight, up_weight, routes):
-    return move(gate_weight, up_weight, routes)
+    return store(*move(gate_weight, up_weight, routes))
 
 
 def solution(mesh):

time: 85.9 us -> 80.3 us (0.935); the launches traced: 84.6 us -> 80 us
  local copies, waits for them, and re-layouts: 5.7 us -> 0 us
  Pallas kernels: 78.3 us -> 79.3 us
    unnamed x7 -> x0, local copies, waits for them, and re-layouts: 5.7 us -> none
    pallas_call x1 -> x2, Pallas kernels: 78.3 us -> 79.3 us  [the longest x1 76.9 us: move(): pl.pallas_call(move_kernel, out_shape=(pltpu.VMEM((2, SIDE, 4608), jnp.bf...]
where the time goes in v3:
time: 80.3 us; the launch traced here: 80 us
  Pallas kernels  79.3 us (99%)
    pallas_call x1, Pallas kernels, move(): pl.pallas_call(move_kernel, out_shape=(pltpu.VMEM((2, SIDE, 4608), jnp.bf...  76.9 us
    pallas_call x1, Pallas kernels, store(): pl.pallas_call(store_kernel, out_shape=(jax.ShapeDtypeStruct((SIDE, 4608)...  2.43 us

profile of v3, /device:TPU:1, one launch (start us, length us, event | category | flops | bytes accessed | tf_op | source)
XLA Modules:
  0.0 80.0 jit_solution(17076741084294609641)
XLA Ops:
  0.6 76.9 %shard_map.58 = (bf16[2,288,4608]{2,1,0:T(8,128)(2,1)S(1)}, f32[2,4608]{1,0:T(2,128)S(1)}) custom-call(s32[2,8]{1,0:T(2,128)} %routes_in.1, bf16[576,2304]{1,0:T(8,128)(2,1)} %gate.1, bf16[576,2304]{1,0:T(8,128)(2,1)} %up.1), custom_call_target="tpu_custom_call" | custom-call | tf_op jit(solution)/shard_map/pallas_call | solution.py:311
  77.5 2.4 %shard_map.59 = (bf16[288,4608]{1,0:T(8,128)(2,1)}, bf16[288,4608]{1,0:T(8,128)(2,1)}, f32[2,4608]{1,0:T(2,128)}) custom-call(bf16[2,288,4608]{2,1,0:T(8,128)(2,1)S(1)} %get-tuple-element.5.final, f32[2,4608]{1,0:T(2,128)S(1)} %get-tuple-element.6.lines), custom_call_target="tpu_custom_call" | custom-call | tf_op jit(solution)/shard_map/pallas_call | solution.py:370

commit v4 on v3

--- a/solution.py
+++ b/solution.py
@@ -121,7 +121,7 @@
 
 def lay_out(blocks, factor, out, p):
     proj = p // PARTS
-    rows = pl.ds(pl.multiple_of((p % PARTS) * PART, PART), PART)
+    rows = pl.ds(p % PARTS * PART, PART) if isinstance(p, int) else pl.ds(pl.multiple_of(p % PARTS * PART, PART), PART)
     for quad in range(4):
         pieces = []
         for i in range(4):
@@ -138,7 +138,7 @@
 
 
 def move_kernel(
-    routes_in, gate, up, final, scales, routes, slab, src, relay, out, packed, line, pieces, peaks, mine, total, gathered, factor,
+    routes_in, gate, up, final, out, scales, factor, routes, slab, src, relay, packed, line, pieces, peaks, mine, total, gathered,
     slab_sems, sends, relay_sems, out_sems, peak_sems, routes_sem
 ):
     x, y, z, k = place()
@@ -171,11 +171,11 @@
         pl.semaphore_signal(barrier, 1, device_id=other, device_id_type=MESH)
 
     def first(hi, zi, dx, p):
-        h, zl = (k + hi) % 2, (z_lo + zi) % 2
+        h, zl = (k + hi) % 2, (z_lo + z_hi + zi) % 2
         xd, zd = (x + dx) % 4, 2 * (x % 2) + zl
         block = src.at[2 * (zl * 4 + xd) + h, p]
         to = device(xd, y, zd, h)
-        at_all = jnp.logical_not(near) if (hi, zi, dx) == (0, 0, 0) else True
+        at_all = jnp.logical_not(jnp.logical_and(near, zl == z_lo)) if (hi, dx) == (0, 0) else True
 
         @pl.when(jnp.logical_and(at_all, stay))
         def _():
@@ -185,15 +185,15 @@
         def _():
             remote(block, relay.at[slot, p], sends.at[0], relay_sems.at[slot, p], to).start()
 
-    def second(hi, zi, a, zs, p):
-        zl, ks = (z_lo + zi) % 2, (k + hi) % 2
+    def second(hi, zi, a, zl, p):
+        zs, ks = (z_lo + zi + zl) % 2, (k + hi) % 2
         yd = 2 * zl + a
         q = zs * 2 + ks
         here = yd * 4 + q
         to = device(x, yd, z, k)
         target = out.at[y * 4 + q, p]
         go = yd != y
-        if (hi, zi) == (0, 0):
+        if hi == 0:
             local = jnp.logical_and(near, jnp.logical_and(yd == goal, zs == z_hi))
 
             @pl.when(jnp.logical_and(go, local))
@@ -209,7 +209,7 @@
 
     groups = [(0, 0), (0, 1), (1, 0), (1, 1)]
     firsts = [(*g, dx) for g in groups for dx in (1, 3, 2, 0)]
-    seconds = [(*g, a, zs) for g in groups for a in range(2) for zs in range(2)]
+    seconds = [(*g, a, zl) for g in groups for zl in range(2) for a in range(2)]
 
     def prepare(p, halves=(0, 1)):
         pack(routes, slab, packed, src, p, halves)
@@ -241,7 +241,10 @@
         def _():
             wait_bytes(out.at[:, p], out_sems.at[p])
 
-        lay_out(out, factor, final, p)
+        @pl.when(p < CHUNKS - 1)
+        def _():
+            lay_out(out, factor, final, p)
+
         return 0
 
     for n in range(2, 2 * CHUNKS):
@@ -312,18 +315,19 @@
         move_kernel,
         out_shape=(
             pltpu.VMEM((2, SIDE, 4608), jnp.bfloat16),
+            pltpu.VMEM(shape, jnp.bfloat16),
             pltpu.VMEM((2, 4608), jnp.float32),
+            pltpu.VMEM((2, 1, 4608), jnp.float32),
         ),
         in_specs=[
             pl.BlockSpec(memory_space=pltpu.HBM),
             pl.BlockSpec(memory_space=pltpu.HBM),
             pl.BlockSpec(memory_space=pltpu.HBM),
         ],
-        out_specs=(pl.BlockSpec(memory_space=pltpu.VMEM),) * 2,
+        out_specs=(pl.BlockSpec(memory_space=pltpu.VMEM),) * 4,
         scratch_shapes=[
             pltpu.SMEM((2, 8), jnp.int32),
             pltpu.VMEM((2 * CHUNKS, PART, 2304), jnp.bfloat16),
-            pltpu.VMEM(shape, jnp.bfloat16),
             pltpu.VMEM(shape, jnp.bfloat16),
             pltpu.VMEM(shape, jnp.bfloat16),
             pltpu.VMEM((16, ROWS, 128), jnp.bfloat16),
@@ -333,7 +337,6 @@
             pltpu.VMEM((8, 8, 128), jnp.float32),
             pltpu.VMEM((8, 128), jnp.float32),
             pltpu.VMEM((16, 8, 128), jnp.float32),
-            pltpu.VMEM((2, 1, 4608), jnp.float32),
             pltpu.SemaphoreType.DMA((2 * CHUNKS,)),
             pltpu.SemaphoreType.DMA((5,)),
             pltpu.SemaphoreType.DMA((16, CHUNKS)),
@@ -351,22 +354,25 @@
     )
 
 
-def store_kernel(final, lines, gate, up, scales, sems):
+def store_kernel(final, blocks, lines, factor, gate, up, scales, last, sems):
     copies = [
         pltpu.make_async_copy(
-            final.at[proj, pl.ds(i * PART, PART)], ref.at[pl.ds(i * PART, PART)], sems.at[proj * PARTS + i]
+            (last if n == CHUNKS - 1 else final).at[n // PARTS, pl.ds(n % PARTS * PART, PART)],
+            (gate, up)[n // PARTS].at[pl.ds(n % PARTS * PART, PART)],
+            sems.at[n],
         )
-        for proj, ref in enumerate((gate, up))
-        for i in range(PARTS)
+        for n in range(CHUNKS)
     ]
-    copies.append(pltpu.make_async_copy(lines, scales, sems.at[2 * PARTS]))
-    for copy in copies:
+    copies.insert(CHUNKS - 1, pltpu.make_async_copy(lines, scales, sems.at[CHUNKS]))
+    for copy in copies[:-1]:
         copy.start()
+    lay_out(blocks, factor, last, CHUNKS - 1)
+    copies[-1].start()
     for copy in copies:
         copy.wait()
 
 
-def store(final, lines):
+def store(*results):
     return pl.pallas_call(
         store_kernel,
         out_shape=(
@@ -374,14 +380,14 @@
             jax.ShapeDtypeStruct((SIDE, 4608), jnp.bfloat16),
             jax.ShapeDtypeStruct((2, 4608), jnp.float32),
         ),
-        in_specs=[pl.BlockSpec(memory_space=pltpu.VMEM)] * 2,
+        in_specs=[pl.BlockSpec(memory_space=pltpu.VMEM)] * 4,
         out_specs=(pl.BlockSpec(memory_space=pltpu.HBM),) * 3,
-        scratch_shapes=[pltpu.SemaphoreType.DMA((2 * PARTS + 1,))],
-        compiler_params=pltpu.CompilerParams(vmem_limit_bytes=2**20),
-    )(
-        pltpu.with_memory_space_constraint(final, pltpu.VMEM),
-        pltpu.with_memory_space_constraint(lines, pltpu.VMEM),
-    )
+        scratch_shapes=[
+            pltpu.VMEM((2, SIDE, 4608), jnp.bfloat16),
+            pltpu.SemaphoreType.DMA((CHUNKS + 1,)),
+        ],
+        compiler_params=pltpu.CompilerParams(vmem_limit_bytes=10 * 2**20),
+    )(*(pltpu.with_memory_space_constraint(result, pltpu.VMEM) for result in results))
 
 
 def shards(gate_weight, up_weight, routes):

time: 80.3 us -> 78.4 us (0.976)
  Pallas kernels: 79.3 us -> 77.2 us
    pallas_call x1, Pallas kernels: 76.9 us -> 74.7 us  [move(): pl.pallas_call(move_kernel, out_shape=(pltpu.VMEM((2, SIDE, 4608), jnp.bf...]
where the time goes in v4:
time: 78.4 us; the launch traced here: 77.8 us
  Pallas kernels  77.2 us (98%)
    pallas_call x1, Pallas kernels, move(): pl.pallas_call(move_kernel, out_shape=(pltpu.VMEM((2, SIDE, 4608), jnp.bf...  74.7 us
    pallas_call x1, Pallas kernels, store(): pl.pallas_call(store_kernel, out_shape=(jax.ShapeDtypeStruct((SIDE, 4608)...  2.44 us

profile of v4, /device:TPU:1, one launch (start us, length us, event | category | flops | bytes accessed | tf_op | source)
XLA Modules:
  0.0 77.8 jit_solution(7644198476066599109)
XLA Ops:
  0.6 74.7 %shard_map.58 = (bf16[2,288,4608]{2,1,0:T(8,128)(2,1)S(1)}, bf16[16,6,216,128]{3,2,1,0:T(8,128)(2,1)S(1)}, f32[2,4608]{1,0:T(2,128)S(1)}, f32[2,1,4608]{2,1,0:T(1,128)S(1)}) custom-call(s32[2,8]{1,0:T(2,128)} %routes_in.1, bf16[576,2304]{1,0:T(8,128)(2,1)} %gate.1, bf16[576,2304]{1,0:T(8,128)(2,1)} %up.1), custom_call_target="tpu_custom_call" | custom-call | tf_op jit(solution)/shard_map/pallas_call | solution.py:314
  75.4 2.4 %shard_map.59 = (bf16[288,4608]{1,0:T(8,128)(2,1)}, bf16[288,4608]{1,0:T(8,128)(2,1)}, f32[2,4608]{1,0:T(2,128)}) custom-call(bf16[2,288,4608]{2,1,0:T(8,128)(2,1)S(1)} %get-tuple-element.7.final, bf16[16,6,216,128]{3,2,1,0:T(8,128)(2,1)S(1)} %get-tuple-element.8.blocks, f32[2,4608]{1,0:T(2,128)S(1)} %get-tuple-element.9.lines, ...), custom_call_target="tpu_custom_call" | custom-call | tf_op jit(solution)/shard_map/pallas_call | solution.py:376

commit v5 on v4

--- a/solution.py
+++ b/solution.py
@@ -278,10 +278,10 @@
     wait_bytes(mine.at[pl.ds(0, 7)], peak_sems.at[0])
     total[...] = jnp.max(mine[...], axis=0)
     gathered[col] = total[...]
-    lax.fori_loop(1, 2, full_round, 0)
     for n in range(1, 4):
         to = device(x, y, (z + 2 * (n // 2)) % 4, (k + n % 2) % 2)
         remote(total, gathered.at[col], sends.at[3], peak_sems.at[1], to).start()
+    lax.fori_loop(1, 2, full_round, 0)
     lax.fori_loop(2, 3, full_round, 0)
     lax.fori_loop(3, 4, full_round, 0)
     wait_bytes(gathered.at[pl.ds(0, 3)], peak_sems.at[1])

time: 78.4 us -> 78.7 us (level)
  no operation moved by 1% of the time
where the time goes in v5:
time: 78.7 us; the launch traced here: 77.9 us
  Pallas kernels  77.2 us (98%)
    pallas_call x1, Pallas kernels, move(): pl.pallas_call(move_kernel, out_shape=(pltpu.VMEM((2, SIDE, 4608), jnp.bf...  74.8 us
    pallas_call x1, Pallas kernels, store(): pl.pallas_call(store_kernel, out_shape=(jax.ShapeDtypeStruct((SIDE, 4608)...  2.44 us

profile of v5, /device:TPU:1, one launch (start us, length us, event | category | flops | bytes accessed | tf_op | source)
XLA Modules:
  0.0 77.9 jit_solution(7450084687216589483)
XLA Ops:
  0.6 74.8 %shard_map.58 = (bf16[2,288,4608]{2,1,0:T(8,128)(2,1)S(1)}, bf16[16,6,216,128]{3,2,1,0:T(8,128)(2,1)S(1)}, f32[2,4608]{1,0:T(2,128)S(1)}, f32[2,1,4608]{2,1,0:T(1,128)S(1)}) custom-call(s32[2,8]{1,0:T(2,128)} %routes_in.1, bf16[576,2304]{1,0:T(8,128)(2,1)} %gate.1, bf16[576,2304]{1,0:T(8,128)(2,1)} %up.1), custom_call_target="tpu_custom_call" | custom-call | tf_op jit(solution)/shard_map/pallas_call | solution.py:314
  75.4 2.4 %shard_map.59 = (bf16[288,4608]{1,0:T(8,128)(2,1)}, bf16[288,4608]{1,0:T(8,128)(2,1)}, f32[2,4608]{1,0:T(2,128)}) custom-call(bf16[2,288,4608]{2,1,0:T(8,128)(2,1)S(1)} %get-tuple-element.7.final, bf16[16,6,216,128]{3,2,1,0:T(8,128)(2,1)S(1)} %get-tuple-element.8.blocks, f32[2,4608]{1,0:T(2,128)S(1)} %get-tuple-element.9.lines, ...), custom_call_target="tpu_custom_call" | custom-call | tf_op jit(solution)/shard_map/pallas_call | solution.py:376
